TPU v7x, 128 devices: a whole 4x4x4 slice. The times are simulated.
128 devices in a mesh: fit: 8 (over z, core), pair: 16 (over x, y).
Axes of the slice: x: 4, y: 4, z: 4, core: 2. Of those that a mesh axis runs over, the one named last changes fastest.
Arguments:
- metric_factor: bfloat16 [4096, 4096], P('fit'), as said below
- three_index: bfloat16 [4096, 32768], P('fit', 'pair'), may hold values from -6 to 6
- send_map: int32 [16, 16, 8], P('pair'), may hold values from 0 to 15
- pair_slots: int32 [16, 128], P('pair'), may hold values from 0 to 127, each once within a row
- pair_count: int32 [16], P('pair'), may hold values from 1 to 64, 512 in all
- orbital_energy: bfloat16 [256], P('pair'), may hold values from -2 to -0.19921875
- cabs_energy: float32 [1024], replicated, may hold values from 0.5 to 4
- coupling: bfloat16 [128, 1024], replicated, may hold values from -0.5 to 0.5
Outputs:
- projected: bfloat16 [16, 64, 128, 1024], P('pair', 'fit')
Inputs may be any that keep to these rules, and one draw needn't show every extreme that they name: `metric_factor`: diagonal entries lie between 0.6 and 1.4. `pair_slots`: each row holds every position 0 to 127 once; pair n of a row uses entries 2n and 2n + 1.
All inputs are finite; a program needn't handle non-finite values. No bound on the sum of `pair_count` on one device may be relied on, other than what follows from the above.
Results may differ from a plain program's by a relative error of at most 0.015.
Values may be sent and summed in bfloat16 or wider, within the bound.
A program may use at most 256 MiB of HBM per device.

v0:
```python
import jax
import jax.numpy as jnp
from jax import lax
from jax.sharding import PartitionSpec as P

NAUX = 4096
PAIR_BLOCK = 8


def turned_gather(arrays, axis, dims):
    turned = [jnp.moveaxis(a, dim, 0) for a, dim in zip(arrays, dims)]
    both = jnp.concatenate([t.reshape(len(t), -1) for t in turned], axis=1)
    filled, at, outs = (lax.all_gather(both, axis, axis=0, tiled=True), 0, [])
    for t, dim in zip(turned, dims):
        slab = filled[:, at : at + t[0].size].reshape(-1, *t.shape[1:])
        outs.append(jnp.moveaxis(slab, 0, dim))
        at += t[0].size
    return tuple(outs)


def on_device(
    metric_factor,
    three_index,
    send_map,
    pair_slots,
    pair_count,
    orbital_energy,
    cabs_energy,
    coupling,
):
    domain = coupling.shape[0]
    orbitals = orbital_energy.shape[0]
    local_rows = metric_factor.shape[0]
    peers = send_map.shape[1]
    capacity = send_map.shape[2]
    slot_total = pair_slots.shape[1] // 2
    fitted = jnp.dot(
        metric_factor,
        lax.all_gather(three_index, "fit", axis=0, tiled=True),
        preferred_element_type=jnp.float32,
    )
    fitted = fitted.astype(jnp.bfloat16).reshape(local_rows, orbitals, domain)
    requests = send_map.reshape(peers, capacity)
    source, energy_src = turned_gather((fitted, orbital_energy), "pair", (1, 0))
    global_ids = (jnp.arange(peers, dtype=jnp.int32)[:, None] * orbitals + requests).reshape(-1)
    pair_index = jnp.take(global_ids, pair_slots[0])
    left_index = pair_index[0::2]
    right_index = pair_index[1::2]
    live_count = pair_count[0]
    norm_scale = NAUX ** (-0.5)
    block_count = (live_count + PAIR_BLOCK - 1) // PAIR_BLOCK

    def advance(block, partial_value):
        left_ids = lax.dynamic_slice_in_dim(left_index, block * PAIR_BLOCK, PAIR_BLOCK)
        right_ids = lax.dynamic_slice_in_dim(right_index, block * PAIR_BLOCK, PAIR_BLOCK)
        left_rows = jnp.take(source, left_ids, axis=1)
        right_rows = jnp.take(source, right_ids, axis=1)
        product = jnp.einsum(
            "qsa,qsb->sab", left_rows, right_rows, preferred_element_type=jnp.float32
        )
        return lax.dynamic_update_slice_in_dim(
            partial_value, product * norm_scale, block * PAIR_BLOCK, 0
        )

    partial_value = jnp.zeros((slot_total, domain, domain), jnp.float32)
    partial_value = lax.fori_loop(0, block_count, advance, partial_value)
    share = slot_total // lax.axis_size("fit")
    first_slot = lax.axis_index("fit") * share
    exchange = lax.psum_scatter(
        partial_value.astype(jnp.bfloat16), "fit", scatter_dimension=0, tiled=True
    )
    energy_sum = jnp.take(energy_src, left_index).astype(jnp.float32) + jnp.take(
        energy_src, right_index
    ).astype(jnp.float32)
    energy_sum = lax.dynamic_slice_in_dim(energy_sum, first_slot, share, 0)
    weighted = jnp.einsum("sab,bc->sac", exchange, coupling, preferred_element_type=jnp.float32)
    denom = cabs_energy[None, None, :] - energy_sum[:, None, None]
    live_mask = first_slot + jnp.arange(share, dtype=jnp.int32) < live_count
    projected = jnp.where(live_mask[:, None, None], weighted / denom, 0.0).astype(jnp.bfloat16)
    return projected.reshape(1, share, domain, weighted.shape[2])


def solution(mesh):
    in_specs = (
        P("fit", None),
        P("fit", "pair"),
        P("pair", None, None),
        P("pair", None),
        P("pair"),
        P("pair"),
        P(),
        P(),
    )
    out_specs = P("pair", "fit", None, None)
    return jax.shard_map(
        on_device, mesh=mesh, in_specs=in_specs, out_specs=out_specs, check_vma=False
    )
```

profile of v0, /device:TPU:0, one launch (start us, length us, event | category | flops | bytes accessed | tf_op | source)
XLA Modules:
  0.0 506.7 jit_solution(18273993454955358155)
XLA Ops:
  8.1 88.6 %all-gather.3.cloned.1.call-done = bf16[4096,2048]{1,0:T(8,128)(2,1)} async-done(((bf16[512,2048]{1,0:T(8,128)(2,1)}), bf16[4096,2048]{1,0:T(8,128)(2,1)}) %all-gather.3.cloned.1.call-update) | async-done | bytes 16777232 | tf_op jit(solution)/shard_map/all_gather | solution.py:39
  96.7 13.6 %fusion.9 = bf16[64,16,8,128]{3,2,1,0:T(8,128)(2,1)S(1)} fusion(bf16[512,4096]{1,0:T(8,128)(2,1)} %param.14, bf16[4096,2048]{1,0:T(8,128)(2,1)} %all-gather.3.cloned.1.call-done), kind=kOutput, calls=%fused_computation.26 | convolution fusion | flops 8590983168 | bytes 23068672 | tf_op jit(solution)/shard_map/dot_general | solution.py:37
  116.4 195.1 %all-gather.5.cloned.1.call-done = bf16[256,65537]{1,0:T(8,128)(2,1)} async-done(((bf16[16,65537]{1,0:T(8,128)(2,1)}), bf16[256,65537]{1,0:T(8,128)(2,1)}) %all-gather.5.cloned.1.call-update) | async-done | bytes 33554960 | tf_op jit(solution)/shard_map/all_gather | solution.py:13
  311.5 22.9 %slice.26 = bf16[256,65536]{1,0:T(8,128)(2,1)} slice(bf16[256,65537]{1,0:T(8,128)(2,1)} %all-gather.5.cloned.1.call-done), slice={[0:256], [0:65536]} | slice | bytes 67108864 | tf_op jit(solution)/shard_map/slice | solution.py:15
  334.3 41.6 %copy.17 = bf16[256,65536]{0,1:T(8,128)(2,1)} copy(bf16[256,65536]{1,0:T(8,128)(2,1)} %slice.26) | data formatting | bytes 67108864 | tf_op jit(solution)/shard_map/slice | solution.py:15
  375.9 43.8 %copy.18 = bf16[512,256,128]{2,0,1:T(8,128)(2,1)} copy(bf16[512,256,128]{1,2,0:T(8,128)(2,1)} %bitcast.41) | data formatting | bytes 67108864 | tf_op jit(solution)/shard_map/while | solution.py:66
  421.5 42.6 %while.10 = (s32[]{:T(128)}, bf16[64,128,128]{2,1,0:T(8,128)(2,1)}, s32[]{:T(128)}, s32[64]{0:T(128)S(1)}, bf16[512,256,128]{2,0,1:T(8,128)(2,1)}, /*index=5*/s3...) while((s32[]{:T(128)}, bf16[64,128,128]{2,1,0:T(8,128)(2,1)}, s32[]{:T(128)}, s32[64]{0:T(128)S(1)}, ...), condition=%wide.region_1.3_spmd, body=%wide.region_0.0_spmd.sunk | while | flops 135399520 | bytes 6824379 | solution.py:66
  421.6 2.0 gather_fusion.1
  423.6 2.0 gather_fusion
  426.9 2.0 gather_fusion.1
  428.9 2.0 gather_fusion
  432.2 2.0 gather_fusion.1
  434.2 2.0 gather_fusion
  437.6 2.0 gather_fusion.1
  439.5 2.0 gather_fusion
  442.9 2.0 gather_fusion.1
  444.9 2.0 gather_fusion
  448.2 2.0 gather_fusion.1
  450.2 2.0 gather_fusion
  453.5 2.0 gather_fusion.1
  455.5 2.0 gather_fusion
  458.9 2.0 gather_fusion.1
  466.8 30.3 %reduce-scatter.2.cloned.1.call-done = bf16[8,128,128]{2,1,0:T(8,128)(2,1)} async-done(((bf16[64,128,128]{2,1,0:T(8,128)(2,1)}), bf16[8,128,128]{2,1,0:T(8,128)(2,1)}) %reduce-scatter.2.cloned.1.call-update) | async-done | bytes 262160 | tf_op jit(solution)/shard_map/reduce_scatter | solution.py:69
  497.2 3.0 fusion.10
  (75 shorter events, 24.4 us)
Async XLA Ops:
  6.5 490.6 %copy-start = (bf16[128,1024]{1,0:T(8,128)(2,1)S(1)}, bf16[128,1024]{1,0:T(8,128)(2,1)}, u32[]{:S(2)}) copy-start(bf16[128,1024]{1,0:T(8,128)(2,1)} %param.21) | copy-start | bytes 786436
  6.5 90.1 %all-gather.3.cloned.1.call-start = ((), (), s32[]{:S(2)}) async-start(), calls=%async_computation.1 | async-start | bytes 18874368 | tf_op jit(solution)/shard_map/all_gather | solution.py:39
  7.3 304.2 %all-gather.5.cloned.1.call-start = ((), (), s32[]{:S(2)}) async-start(), calls=%async_computation.2 | async-start | bytes 35721216 | tf_op jit(solution)/shard_map/all_gather | solution.py:13
  112.2 2.4 copy-start.1
  112.2 2.6 copy-start.3
  113.7 383.5 %reduce-scatter.2.cloned.1.call-start = ((), (), s32[]{:S(2)}) async-start(), calls=%async_computation.3 | async-start | bytes 2359296 | tf_op jit(solution)/shard_map/reduce_scatter | solution.py:69
  421.5 45.3 %copy-start.2 = (f32[1024]{0:T(1024)S(1)}, f32[1024]{0:T(1024)}, u32[]{:S(2)}) copy-start(f32[1024]{0:T(1024)} %param.20) | copy-start | bytes 12292
Sparse Core Ops, SparseCore 0:
  9.0 87.5 all-gather.2
  113.8 197.6 all-gather.4
  464.2 32.9 reduce-scatter.1
where the time goes:
time: 509 us; the launch traced here: 507 us
  waiting for transfers between devices  315 us (62%)
  local copies, waits for them, and re-layouts  149 us (29%)
  matrix products  26.9 us (5%)
  between operations  13.9 us (3%)
    all_gather x1, waiting for transfers between devices, turned_gather(): filled, at, outs = (lax.all_gather(both, axis, axis=0, tiled=True), 0, [])  195 us
    all_gather x1, waiting for transfers between devices, on_device(): lax.all_gather(three_index, 'fit', axis=0, tiled=True)  88.6 us
    slice x3, local copies, waits for them, and re-layouts, turned_gather(): slab = filled[:, at:at + t[0].size].reshape(-1, *t.shape[1:])  65.4 us
    while x1, local copies, waits for them, and re-layouts, on_device(): partial_value = lax.fori_loop(0, block_count, advance, partial_value)  43.8 us
    reduce_scatter x1, waiting for transfers between devices, on_device(): lax.psum_scatter(partial_value.astype(jnp.bfloat16), 'fit', scatter_dimen...  30.3 us
    gather x8, local copies, waits for them, and re-layouts, advance(): left_rows = jnp.take(source, left_ids, axis=1)  15.7 us
    gather x8, local copies, waits for them, and re-layouts, advance(): right_rows = jnp.take(source, right_ids, axis=1)  15.7 us
    dot_general x1, matrix products, on_device(): jnp.dot(metric_factor, lax.all_gather(three_index, 'fit', axis=0, tiled=T...  13.6 us
  transfers between devices with their start and end apart: 3, of which 3 were waited for; matrix products, arithmetic and copies ran while one was open for 1% of the time, Pallas kernels for 0%

commit v1 on v0

--- a/solution.py
+++ b/solution.py
@@ -5,6 +5,38 @@
 
 NAUX = 4096
 PAIR_BLOCK = 8
+
+
+def _supply_wires(tile_in, dim_no):
+    tile_in = jnp.moveaxis(tile_in, 0, dim_no)
+    a_next = tile_in.shape
+    latest = tile_in.reshape(
+        *a_next[:dim_no], a_next[dim_no] * a_next[dim_no + 1], *a_next[dim_no + 2 :]
+    )
+    return latest
+
+
+def time_numbers(local_x, comm_axis, at_axis):
+    n_chips = lax.axis_size(comm_axis)
+    current_value = map(lambda tick: (tick, (tick + 1) % n_chips), range(n_chips))
+    items = list(current_value)
+    mat_out, local_next = ([], [])
+    in_order = [(j, k0) for k0, j in items]
+    for rr in range(n_chips - 1):
+        if rr % 2 == 0:
+            vec_out = lax.ppermute(mat_out[-1] if mat_out else local_x, comm_axis, items)
+            mat_out.append(vec_out)
+        else:
+            local_next.append(
+                lax.ppermute(local_next[-1] if local_next else local_x, comm_axis, in_order)
+            )
+    outer = jnp.stack([*mat_out[::-1], local_x, *local_next], axis=0)
+    part_now = len(mat_out)
+    d_next = lax.axis_index(comm_axis)
+    w1 = d_next - part_now
+    outer = outer[(jnp.arange(n_chips) - w1) % n_chips]
+    v_next = _supply_wires(outer, at_axis)
+    return v_next
 
 
 def turned_gather(arrays, axis, dims):
@@ -35,9 +67,7 @@
     capacity = send_map.shape[2]
     slot_total = pair_slots.shape[1] // 2
     fitted = jnp.dot(
-        metric_factor,
-        lax.all_gather(three_index, "fit", axis=0, tiled=True),
-        preferred_element_type=jnp.float32,
+        metric_factor, time_numbers(three_index, "fit", 0), preferred_element_type=jnp.float32
     )
     fitted = fitted.astype(jnp.bfloat16).reshape(local_rows, orbitals, domain)
     requests = send_map.reshape(peers, capacity)

time: 509 us -> 570 us (1.12)
  local copies, waits for them, and re-layouts: 149 us -> 185 us
  starting transfers between devices: 0.08 us -> 9.11 us
  other arithmetic: 2.32 us -> 10.1 us
  waiting for transfers between devices: 315 us -> 322 us
    ppermute x0 -> x7, waiting for transfers between devices: none -> 98.3 us  [the longest x4 98.3 us: time_numbers(): lax.ppermute(mat_out[-1] if mat_out else local_x, comm_axis, items)]
    all_gather x1 -> x0, waiting for transfers between devices: 88.6 us -> none  [on_device(): lax.all_gather(three_index, 'fit', axis=0, tiled=True)]
    gather x0 -> x3, local copies, waits for them, and re-layouts: none -> 22.6 us  [time_numbers(): outer = outer[(jnp.arange(n_chips) - w1) % n_chips]]
    unnamed x10 -> x23, local copies, waits for them, and re-layouts: 1.45 us -> 10.5 us
    ppermute x0 -> x7, starting transfers between devices: none -> 8.88 us  [the longest x3 8.87 us: time_numbers(): lax.ppermute(local_next[-1] if local_next else local_x, comm_axis, in_order)]
    unnamed x0 -> x1, other arithmetic: none -> 7.8 us
  transfers between devices with their start and end apart: 3 -> 9, of which waited for: 3 -> 6; matrix products, arithmetic and copies ran while one was open for 1% -> 2% of each run, Pallas kernels for 0% -> 0%
where the time goes in v1:
time: 570 us; the launch traced here: 567 us
  waiting for transfers between devices  322 us (56%)
  local copies, waits for them, and re-layouts  185 us (32%)
  matrix products  26.4 us (5%)
  between operations  14.3 us (3%)
  other arithmetic  10.1 us (2%)
  starting transfers between devices  9.11 us (2%)
    all_gather x1, waiting for transfers between devices, turned_gather(): filled, at, outs = (lax.all_gather(both, axis, axis=0, tiled=True), 0, [])  193 us
    ppermute x4, waiting for transfers between devices, time_numbers(): lax.ppermute(mat_out[-1] if mat_out else local_x, comm_axis, items)  98.3 us
    slice x3, local copies, waits for them, and re-layouts, turned_gather(): slab = filled[:, at:at + t[0].size].reshape(-1, *t.shape[1:])  67.6 us
    while x1, local copies, waits for them, and re-layouts, on_device(): partial_value = lax.fori_loop(0, block_count, advance, partial_value)  43.7 us
    reduce_scatter x1, waiting for transfers between devices, on_device(): lax.psum_scatter(partial_value.astype(jnp.bfloat16), 'fit', scatter_dimen...  30.3 us
    gather x3, local copies, waits for them, and re-layouts, time_numbers(): outer = outer[(jnp.arange(n_chips) - w1) % n_chips]  22.6 us
    gather x8, local copies, waits for them, and re-layouts, advance(): left_rows = jnp.take(source, left_ids, axis=1)  15.7 us
    gather x8, local copies, waits for them, and re-layouts, advance(): right_rows = jnp.take(source, right_ids, axis=1)  15.7 us
  transfers between devices with their start and end apart: 9, of which 6 were waited for; matrix products, arithmetic and copies ran while one was open for 2% of the time, Pallas kernels for 0%

profile of v1, /device:TPU:0, one launch (start us, length us, event | category | flops | bytes accessed | tf_op | source)
XLA Modules:
  0.0 567.1 jit_solution(15928805245073289172)
XLA Ops:
  6.5 27.5 %collective-permute-done = bf16[512,2048]{1,0:T(8,128)(2,1)S(1)} collective-permute-done((bf16[512,2048]{1,0:T(8,128)(2,1)}, bf16[512,2048]{1,0:T(8,128)(2,1)S(1)}, u32[]{:S(2)}, u32[]{:S(2)}) %collective-permute-start) | collective-permute-done | bytes 2097184 | tf_op jit(solution)/shard_map/ppermute | solution.py:27
  34.1 3.0 collective-permute-start.4
  37.0 23.7 %collective-permute-done.1 = bf16[512,2048]{1,0:T(8,128)(2,1)S(1)} collective-permute-done((bf16[512,2048]{1,0:T(8,128)(2,1)S(1)}, bf16[512,2048]{1,0:T(8,128)(2,1)S(1)}, u32[]{:S(2)}, u32[]{:S(2)}) %collective-permute-start.1) | collective-permute-done | bytes 2097184 | tf_op jit(solution)/shard_map/ppermute | solution.py:27
  62.1 3.0 collective-permute-start.5
  65.0 23.8 %collective-permute-done.2 = bf16[512,2048]{1,0:T(8,128)(2,1)} collective-permute-done((bf16[512,2048]{1,0:T(8,128)(2,1)S(1)}, bf16[512,2048]{1,0:T(8,128)(2,1)}, u32[]{:S(2)}, u32[]{:S(2)}) %collective-permute-start.2) | collective-permute-done | bytes 2097184 | tf_op jit(solution)/shard_map/ppermute | solution.py:27
  89.6 3.0 collective-permute-start.6
  92.6 23.2 %collective-permute-done.3 = bf16[512,2048]{1,0:T(8,128)(2,1)} collective-permute-done((bf16[512,2048]{1,0:T(8,128)(2,1)}, bf16[512,2048]{1,0:T(8,128)(2,1)}, u32[]{:S(2)}, u32[]{:S(2)}) %collective-permute-start.3) | collective-permute-done | bytes 2097184 | tf_op jit(solution)/shard_map/ppermute | solution.py:27
  123.8 6.4 %fusion.14 = (bf16[8,512,1024]{2,1,0:T(8,128)(2,1)}, bf16[8,512,1024]{2,1,0:T(8,128)(2,1)}) fusion(bf16[8,512,2048]{2,1,0:T(8,128)(2,1)S(1)} %bitcast_dynamic-update-slice_fusion), kind=kLoop, calls=%fused_computation.61 | loop fusion | bytes 33554432 | tf_op jit(solution)/shard_map/gather | solution.py:37
  130.2 8.1 %gather_fusion.3 = bf16[8,512,1024]{2,1,0:T(8,128)(2,1)} fusion(bf16[8,512,1024]{2,1,0:T(8,128)(2,1)} %get-tuple-element.65, s32[1024]{0:T(1024)S(1)} %pad_clamp_fusion.4), kind=kCustom, calls=%fused_computation.5 | custom fusion | bytes 16777248 | tf_op jit(solution)/shard_map/gather | solution.py:37
  138.3 8.1 %gather_fusion.4 = bf16[8,512,1024]{2,1,0:T(8,128)(2,1)} fusion(bf16[8,512,1024]{2,1,0:T(8,128)(2,1)} %get-tuple-element.66, s32[1024]{0:T(1024)S(1)} %pad_clamp_fusion.4), kind=kCustom, calls=%fused_computation.6 | custom fusion | bytes 16777248 | tf_op jit(solution)/shard_map/gather | solution.py:37
  146.3 7.8 %pad_maximum_fusion = bf16[8,512,2048]{2,1,0:T(8,128)(2,1)S(1)} fusion(bf16[8,512,1024]{2,1,0:T(8,128)(2,1)} %gather_fusion.4, bf16[8,512,1024]{2,1,0:T(8,128)(2,1)} %gather_fusion.3), kind=kLoop, calls=%fused_computation.23 | loop fusion | flops 33554432 | bytes 33554432
  154.2 13.2 %convolution_convert_fusion = bf16[2048,512]{1,0:T(8,128)(2,1)} fusion(bf16[4096,2048]{1,0:T(8,128)(2,1)S(1)} %bitcast.59, bf16[512,4096]{1,0:T(8,128)(2,1)} %param.14), kind=kOutput, calls=%fused_computation.25 | convolution fusion | flops 8590983168 | bytes 23068672 | tf_op jit(solution)/shard_map/dot_general | solution.py:69
  167.3 3.1 copy.15
  176.1 193.4 %all-gather.2.cloned.1.call-done = bf16[256,65537]{1,0:T(8,128)(2,1)} async-done(((bf16[16,65537]{1,0:T(8,128)(2,1)}), bf16[256,65537]{1,0:T(8,128)(2,1)}) %all-gather.2.cloned.1.call-update) | async-done | bytes 33554960 | tf_op jit(solution)/shard_map/all_gather | solution.py:45
  369.4 22.8 %slice.30 = bf16[256,65536]{1,0:T(8,128)(2,1)} slice(bf16[256,65537]{1,0:T(8,128)(2,1)} %all-gather.2.cloned.1.call-done), slice={[0:256], [0:65536]} | slice | bytes 67108864 | tf_op jit(solution)/shard_map/slice | solution.py:47
  392.3 43.8 %copy.17 = bf16[256,65536]{0,1:T(8,128)(2,1)} copy(bf16[256,65536]{1,0:T(8,128)(2,1)} %slice.30) | data formatting | bytes 67108864 | tf_op jit(solution)/shard_map/slice | solution.py:47
  436.1 43.7 %copy.18 = bf16[512,256,128]{2,0,1:T(8,128)(2,1)} copy(bf16[512,256,128]{1,2,0:T(8,128)(2,1)} %bitcast.58) | data formatting | bytes 67108864 | tf_op jit(solution)/shard_map/while | solution.py:96
  481.6 42.6 %while.10 = (s32[]{:T(128)}, bf16[64,128,128]{2,1,0:T(8,128)(2,1)}, s32[]{:T(128)}, s32[64]{0:T(128)S(1)}, bf16[512,256,128]{2,0,1:T(8,128)(2,1)}, /*index=5*/s3...) while((s32[]{:T(128)}, bf16[64,128,128]{2,1,0:T(8,128)(2,1)}, s32[]{:T(128)}, s32[64]{0:T(128)S(1)}, ...), condition=%wide.region_1.3_spmd, body=%wide.region_0.2_spmd.sunk | while | flops 135399520 | bytes 6824379 | solution.py:96
  503.0 2.0 gather_fusion.1
  505.0 2.0 gather_fusion
  519.0 2.0 gather_fusion.1
  520.9 2.0 gather_fusion
  527.0 30.3 %reduce-scatter.2.cloned.1.call-done = bf16[8,128,128]{2,1,0:T(8,128)(2,1)} async-done(((bf16[64,128,128]{2,1,0:T(8,128)(2,1)}), bf16[8,128,128]{2,1,0:T(8,128)(2,1)}) %reduce-scatter.2.cloned.1.call-update) | async-done | bytes 262160 | tf_op jit(solution)/shard_map/reduce_scatter | solution.py:99
  557.3 3.0 fusion.9
  (105 shorter events, 54.0 us)
Async XLA Ops:
  6.5 550.8 %copy-start = (bf16[128,1024]{1,0:T(8,128)(2,1)S(1)}, bf16[128,1024]{1,0:T(8,128)(2,1)}, u32[]{:S(2)}) copy-start(bf16[128,1024]{1,0:T(8,128)(2,1)} %param.21) | copy-start | bytes 786436
  6.5 362.9 %all-gather.2.cloned.1.call-start = ((), (), s32[]{:S(2)}) async-start(), calls=%async_computation.1 | async-start | bytes 35721216 | tf_op jit(solution)/shard_map/all_gather | solution.py:45
  6.5 27.5 %collective-permute-start = (bf16[512,2048]{1,0:T(8,128)(2,1)}, bf16[512,2048]{1,0:T(8,128)(2,1)S(1)}, u32[]{:S(2)}, u32[]{:S(2)}) collective-permute-start(bf16[512,2048]{1,0:T(8,128)(2,1)} %param.15), channel_id=1, source_target_pairs={{0,16},{16,32},{32,48},{48,64},{64,80},{80,96},{96,112},{112,0},{1... | collective-permute-start | bytes 6291464 | tf_op jit(solution)/shard_map/ppermute | solution.py:27
  34.1 26.7 %collective-permute-start.1 = (bf16[512,2048]{1,0:T(8,128)(2,1)S(1)}, bf16[512,2048]{1,0:T(8,128)(2,1)S(1)}, u32[]{:S(2)}, u32[]{:S(2)}) collective-permute-start(bf16[512,2048]{1,0:T(8,128)(2,1)S(1)} %collective-permute-done), channel_id=1, source_target_pairs={{0,16},{16,32},{32,48},{48,64},{64,80},{80,96},{96,112},{112,0},{1... | collective-permute-start | bytes 6291464 | tf_op jit(solution)/shard_map/ppermute | solution.py:27
  34.1 28.0 %collective-permute-start.4 = (bf16[512,2048]{1,0:T(8,128)(2,1)}, bf16[512,2048]{1,0:T(8,128)(2,1)}, u32[]{:S(2)}, u32[]{:S(2)}) collective-permute-start(bf16[512,2048]{1,0:T(8,128)(2,1)} %param.15), channel_id=1, source_target_pairs={{16,0},{32,16},{48,32},{64,48},{80,64},{96,80},{112,96},{0,112},{1... | collective-permute-start | bytes 6291464 | tf_op jit(solution)/shard_map/ppermute | solution.py:31
  60.7 1.3 copy-start.2
  62.0 26.8 %collective-permute-start.2 = (bf16[512,2048]{1,0:T(8,128)(2,1)S(1)}, bf16[512,2048]{1,0:T(8,128)(2,1)}, u32[]{:S(2)}, u32[]{:S(2)}) collective-permute-start(bf16[512,2048]{1,0:T(8,128)(2,1)S(1)} %collective-permute-done.1), channel_id=1, source_target_pairs={{0,16},{16,32},{32,48},{48,64},{64,80},{80,96},{96,112},{112,0},{1... | collective-permute-start | bytes 6291464 | tf_op jit(solution)/shard_map/ppermute | solution.py:27
  62.1 27.6 %collective-permute-start.5 = (bf16[512,2048]{1,0:T(8,128)(2,1)}, bf16[512,2048]{1,0:T(8,128)(2,1)}, u32[]{:S(2)}, u32[]{:S(2)}) collective-permute-start(bf16[512,2048]{1,0:T(8,128)(2,1)} %collective-permute-done.4), channel_id=1, source_target_pairs={{16,0},{32,16},{48,32},{64,48},{80,64},{96,80},{112,96},{0,112},{1... | collective-permute-start | bytes 6291464 | tf_op jit(solution)/shard_map/ppermute | solution.py:31
  88.8 27.0 %collective-permute-start.3 = (bf16[512,2048]{1,0:T(8,128)(2,1)}, bf16[512,2048]{1,0:T(8,128)(2,1)}, u32[]{:S(2)}, u32[]{:S(2)}) collective-permute-start(bf16[512,2048]{1,0:T(8,128)(2,1)} %collective-permute-done.2), channel_id=1, source_target_pairs={{0,16},{16,32},{32,48},{48,64},{64,80},{80,96},{96,112},{112,0},{1... | collective-permute-start | bytes 6291464 | tf_op jit(solution)/shard_map/ppermute | solution.py:27
  89.6 29.9 %copy-start.3 = (bf16[512,2048]{1,0:T(8,128)(2,1)S(1)}, bf16[512,2048]{1,0:T(8,128)(2,1)}, u32[]{:S(2)}) copy-start(bf16[512,2048]{1,0:T(8,128)(2,1)} %copy-done.2) | copy-start | bytes 6291460
  89.6 30.2 %copy-start.1 = (bf16[512,2048]{1,0:T(8,128)(2,1)S(1)}, bf16[512,2048]{1,0:T(8,128)(2,1)}, u32[]{:S(2)}) copy-start(bf16[512,2048]{1,0:T(8,128)(2,1)} %param.15) | copy-start | bytes 6291460
  89.6 34.0 %collective-permute-start.6 = (bf16[512,2048]{1,0:T(8,128)(2,1)}, bf16[512,2048]{1,0:T(8,128)(2,1)S(1)}, u32[]{:S(2)}, u32[]{:S(2)}) collective-permute-start(bf16[512,2048]{1,0:T(8,128)(2,1)} %collective-permute-done.5), channel_id=1, source_target_pairs={{16,0},{32,16},{48,32},{64,48},{80,64},{96,80},{112,96},{0,112},{1... | collective-permute-start | bytes 6291464 | tf_op jit(solution)/shard_map/ppermute | solution.py:31
  167.3 6.9 %copy-start.4 = (s32[1,16,8]{1,2,0:T(8,128)S(1)}, s32[1,16,8]{1,2,0:T(8,128)}, u32[]{:S(2)}) copy-start(s32[1,16,8]{1,2,0:T(8,128)} %param.16) | copy-start | bytes 1540
  167.3 7.1 %copy-start.6 = (s32[1,128]{1,0:T(1,128)S(1)}, s32[1,128]{1,0:T(1,128)}, u32[]{:S(2)}) copy-start(s32[1,128]{1,0:T(1,128)} %param.17) | copy-start | bytes 1540
  173.2 384.1 %reduce-scatter.2.cloned.1.call-start = ((), (), s32[]{:S(2)}) async-start(), calls=%async_computation.2 | async-start | bytes 2359296 | tf_op jit(solution)/shard_map/reduce_scatter | solution.py:99
  481.6 45.3 %copy-start.5 = (f32[1024]{0:T(1024)S(1)}, f32[1024]{0:T(1024)}, u32[]{:S(2)}) copy-start(f32[1024]{0:T(1024)} %param.20) | copy-start | bytes 12292
Sparse Core Ops, SparseCore 0:
  173.3 196.0 all-gather.1
  524.3 32.9 reduce-scatter.1
